TPU v7x, 256 devices: a whole 4x4x8 slice. The times are simulated.
256 devices in a mesh: stream: 64 (over x, z, y_hi), span: 4 (over y_lo, core).
Axes of the slice: x: 4, y: 4 (y_hi: 2, y_lo: 2; y = y_hi * 2 + y_lo), z: 8, core: 2. Of those that a mesh axis runs over, the one named last changes fastest.
Arguments:
- state: float32 [2560, 8, 625], P('stream', 'span'), may hold values from -0.25 to 2.5, as said below
- direction: float32 [2560, 8, 625], P('stream', 'span'), may hold values from -6 to 6
- metric: float32 [2560, 8, 3], P('stream', 'span'), may hold values from 1 to 4
- face_source: int32 [2560, 4], P('stream'), may hold values from -1 to 225, as said below
- send_rows: int32 [64, 2, 33], P('stream'), may hold values from 0 to 159, as said below
Outputs:
- residual: float32 [2560, 8, 625], P('stream', 'span')
- basis_next: float32 [2560, 8, 625], P('stream', 'span')
- krylov: float32 [3], replicated
Inputs may be any that keep to these rules, and one draw needn't show every extreme that they name: `state`: conserved variables from density 0.75 to 1.25, flow-wise velocity 0.1 to 0.5, other velocities -0.2 to 0.2, pressure 0.5 to 0.9, so pressure and temperature are positive. `face_source`: the plane is a grid of columns of 32 cells, numbered column by column, partition d owning cells d * 40 to (d + 1) * 40 - 1 in a random local order; flow-wise faces wrap around. Every face neighbour lies in the same or an adjacent partition; -1 stands exactly on the lower face of the lowest and the upper face of the highest row; indices into received blocks point at used slots. `send_rows`: at most 33 faces per neighbouring pair, and some pair uses all 33; slots beyond a pair's count hold 0; the order of slots is the order in which the receiver's face_source refers to them.
All inputs are finite; a program needn't handle non-finite values.
Results may differ from a plain program's by a relative error of at most 0.0003.
Values sent between devices are 32-bit elements.
A program may use at most 128 MiB of HBM per device.

v0:
```python
import math

import jax
import jax.numpy as jnp
import numpy as np
from jax import lax
from jax.experimental import pallas as pl
from jax.experimental.pallas import tpu as pltpu
from jax.sharding import PartitionSpec as P

MESH = pl.DeviceIdType.MESH
F32 = jnp.float32
BF16 = jnp.bfloat16

GAMMA = 1.4
VISC = 0.01
COND = VISC * GAMMA / ((GAMMA - 1.0) * 0.72)

COLS = 40
LAYERS = 2
ROWS = COLS * LAYERS
SLOTS = 33
CHUNK = 8
STRIDES = (25, 5, 1)
GROUP = 16


def diff_table():
    spread = math.sqrt(3.0 / 7.0)
    points = np.array([-1.0, -spread, 0.0, spread, 1.0])
    weights = np.array(
        [
            np.prod([points[row_at] - points[other] for other in range(5) if other != row_at])
            for row_at in range(5)
        ]
    )
    matrix = np.zeros((5, 5))
    for row_at in range(5):
        for col_at in range(5):
            if row_at != col_at:
                matrix[row_at, col_at] = weights[row_at] / (
                    weights[col_at] * (points[row_at] - points[col_at])
                )
        matrix[row_at, row_at] = np.sum(
            [1.0 / (points[row_at] - points[other]) for other in range(5) if other != row_at]
        )
    return matrix


def operator_table():
    line = diff_table()
    line[0, 0] += 5.0
    line[4, 4] -= 5.0
    eye = np.eye(5)
    full = np.zeros((128, 384), np.float32)
    for axis in range(3):
        parts = [eye, eye, eye]
        parts[axis] = line
        volume = np.kron(np.kron(parts[0], parts[1]), parts[2])
        full[:125, axis * 128 : axis * 128 + 125] = volume.T
    high = full.astype(jnp.bfloat16)
    low = (full - high.astype(np.float32)).astype(jnp.bfloat16)
    return np.concatenate([high, high, low], axis=0)


def lane_table():
    table = np.zeros((8, 128), np.float32)
    lanes = np.arange(125)
    for axis, stride in enumerate(STRIDES):
        digit = (lanes // stride) % 5
        table[axis] = 9.0
        table[axis, :125] = digit
        table[3 + axis, :125] = 5.0 * (digit == 4) - 5.0 * (digit == 0)
    table[6, :125] = 1.0
    return table


def roll(value, shift):
    shift %= 128
    return value if shift == 0 else pltpu.roll(value, shift, 1)


def split2(value):
    high = value.astype(BF16)
    return high, (value - high.astype(F32)).astype(BF16)


def split3(value):
    high = value.astype(BF16)
    rest = value - high.astype(F32)
    mid = rest.astype(BF16)
    return high, mid, (rest - mid.astype(F32)).astype(BF16)


def dot(a, b):
    return lax.dot_general(a, b, (((1,), (0,)), ((), ())), preferred_element_type=F32)


def primitive(u, du):
    r = 1.0 / u[0]
    v = [u[1 + i] * r for i in range(3)]
    dv = [(du[1 + i] - v[i] * du[0]) * r for i in range(3)]
    vm = u[1] * v[0] + u[2] * v[1] + u[3] * v[2]
    p = (GAMMA - 1.0) * (u[4] - 0.5 * vm)
    vdm = v[0] * du[1] + v[1] * du[2] + v[2] * du[3]
    vv = v[0] * v[0] + v[1] * v[1] + v[2] * v[2]
    dp = (GAMMA - 1.0) * (du[4] - vdm + 0.5 * vv * du[0])
    t = p * r
    dt = (dp - t * du[0]) * r
    s2 = vv + GAMMA * t
    ds2 = 2.0 * (v[0] * dv[0] + v[1] * dv[1] + v[2] * dv[2]) + GAMMA * dt
    return v, p, t, dv, dp, dt, s2, ds2


def inviscid(u, du, v, p, dv, dp, axis):
    flux = [u[1 + axis]]
    tangent = [du[1 + axis]]
    for i in range(3):
        f = u[1 + i] * v[axis]
        df = du[1 + i] * v[axis] + u[1 + i] * dv[axis]
        if i == axis:
            f = f + p
            df = df + dp
        flux.append(f)
        tangent.append(df)
    flux.append((u[4] + p) * v[axis])
    tangent.append((du[4] + dp) * v[axis] + (u[4] + p) * dv[axis])
    return flux, tangent


def stress(q):
    third = (2.0 / 3.0) * (q[0][0] + q[1][1] + q[2][2])
    tau = [[None] * 3 for _ in range(3)]
    for a in range(3):
        tau[a][a] = VISC * (2.0 * q[a][a] - third)
        for b in range(a + 1, 3):
            tau[a][b] = tau[b][a] = VISC * (q[a][b] + q[b][a])
    return tau


def kernel(
    state_ref,
    dir_ref,
    met_ref,
    fs_ref,
    sr_ref,
    op_ref,
    lane_ref,
    res_ref,
    bas_ref,
    kry_ref,
    x_s,
    u_s,
    w_s,
    c_s,
    m_s,
    fy_s,
    oo_s,
    or_s,
    tab_s,
    zp_s,
    zv_s,
    sb1,
    sb2,
    rx1,
    rx2,
    zs1,
    zs2,
    rz1,
    rz2,
    g_s,
    q_s,
    o_s,
    po_s,
    v_s,
    h_s,
    r_s,
    rs_s,
    y_s,
    acc_s,
    pt_s,
    pb_s,
    ar_a,
    ar_b,
    xs_send,
    xs_recv,
    as_send,
    as_recv,
    bs_send,
    bs_recv,
):
    s = lax.axis_index("stream")
    p = lax.axis_index("span")
    n_s, n_p = 64, 4
    s_lo, s_hi = lax.rem(s + n_s - 1, n_s), lax.rem(s + 1, n_s)
    p_lo, p_hi = lax.rem(p + n_p - 1, n_p), lax.rem(p + 1, n_p)
    quad = 4 * (s // 4)
    mine_a = p * 4 + lax.rem(s, 4)
    mine_b = s // 4

    def peer_a(k):
        j = lax.rem(mine_a + k, GROUP)
        return {"stream": quad + lax.rem(j, 4), "span": j // 4}, j

    def peer_b(k):
        j = lax.rem(mine_b + k, GROUP)
        return {"stream": 4 * j + lax.rem(s, 4), "span": p}, j

    barrier = pltpu.get_barrier_semaphore()

    def greet(target):
        pl.semaphore_signal(barrier, inc=1, device_id=target, device_id_type=MESH)

    greet({"stream": s_lo, "span": p})
    greet({"stream": s_hi, "span": p})
    greet({"stream": s, "span": p_lo})
    greet({"stream": s, "span": p_hi})
    for k in range(1, GROUP):
        greet(peer_a(k)[0])
        greet(peer_b(k)[0])

    lane = lax.broadcasted_iota(jnp.int32, (CHUNK, 128), 1)
    digit = [jnp.broadcast_to(lane_ref[a : a + 1, :], (CHUNK, 128)) for a in range(3)]
    sgn = [jnp.broadcast_to(lane_ref[3 + a : 4 + a, :], (CHUNK, 128)) for a in range(3)]
    node = lane < 125

    for l in range(LAYERS):
        x_s[0, l * COLS : (l + 1) * COLS, 0:625] = state_ref[:, l, :]
        x_s[1, l * COLS : (l + 1) * COLS, 0:625] = dir_ref[:, l, :]

    def pack(fields, axis, upper):
        base = 4 if upper else 0
        acc = None
        for v, field in enumerate(fields):
            moved = roll(field, (v - base) * STRIDES[axis])
            acc = moved if acc is None else jnp.where(digit[axis] == float(v), moved, acc)
        return acc

    def pack_faces(fields, pt, l, rc):
        col = (pt * LAYERS + l) * 128
        for f in range(4):
            tab_s[pl.ds(f * COLS + rc, CHUNK), col : col + 128] = pack(fields, f // 2, f % 2)
        for f in range(2):
            zp_s[f, l, pt, pl.ds(rc, CHUNK), :] = pack(fields, 2, f)

    def each_chunk(body):
        for l in range(LAYERS):

            def step(i, carry, l=l):
                rc = pl.multiple_of(i * CHUNK, CHUNK)
                body(l, rc, pl.multiple_of(l * COLS + rc, CHUNK))
                return carry

            lax.fori_loop(0, COLS // CHUNK, step, 0)

    def first(l, rc, row):
        for pt in range(2):
            tiles = [x_s[pt, pl.ds(row, CHUNK), 128 * t : 128 * t + 128] for t in range(5)]
            fields = []
            for v in range(5):
                value = roll(tiles[v], 3 * v)
                if v:
                    value = jnp.where(lane < 3 * v, roll(tiles[v - 1], 3 * v), value)
                idle = 1.0 if pt == 0 and v in (0, 4) else 0.0
                value = jnp.where(node, value, idle)
                u_s[pt * 5 + v, pl.ds(row, CHUNK), :] = value
                fields.append(value)
            pack_faces(fields, pt, l, rc)

    each_chunk(first)

    eye = lax.broadcasted_iota(jnp.int32, (COLS, COLS), 0) == lax.broadcasted_iota(
        jnp.int32, (COLS, COLS), 1
    )

    def column(row):
        return jnp.sum(
            jnp.where(eye, jnp.broadcast_to(row, (COLS, COLS)), 0.0), axis=1, keepdims=True
        )

    k_own = lax.broadcasted_iota(jnp.int32, (COLS, 160), 1)
    g_own = (
        jnp.where(k_own >= 40, 159, 0)
        + jnp.where(k_own >= 80, 159, 0)
        + jnp.where(k_own >= 120, 159, 0)
    )
    own_id = (4 * k_own - g_own).astype(F32)
    k_rec = lax.broadcasted_iota(jnp.int32, (COLS, 80), 1)
    rec_id = jnp.where(
        k_rec < SLOTS,
        k_rec + 160,
        jnp.where((k_rec >= COLS) & (k_rec < COLS + SLOTS), k_rec + 153, -5),
    ).astype(F32)
    sends = []
    for side in range(2):
        ids = sr_ref[side : side + 1, :].astype(F32)
        slot = lax.broadcasted_iota(jnp.int32, (COLS, SLOTS), 0) == lax.broadcasted_iota(
            jnp.int32, (COLS, SLOTS), 1
        )
        col = jnp.sum(
            jnp.where(slot, jnp.broadcast_to(ids, (COLS, SLOTS)), 0.0), axis=1, keepdims=True
        )
        sends.append(jnp.where(col == own_id, 1.0, 0.0))
    send_hot = jnp.concatenate(sends, axis=0).astype(BF16)

    def remote(src, dst, sem, target):
        return pltpu.make_async_remote_copy(
            src_ref=src,
            dst_ref=dst,
            send_sem=xs_send.at[sem],
            recv_sem=xs_recv.at[sem],
            device_id=target,
            device_id_type=MESH,
        )

    def exchange(sb, rx, zs, rz, base):
        return [
            remote(zs.at[0], rz.at[1], base, {"stream": s, "span": p_lo}),
            remote(zs.at[1], rz.at[0], base + 1, {"stream": s, "span": p_hi}),
            remote(sb.at[pl.ds(0, COLS)], rx.at[pl.ds(COLS, COLS)], base + 2, {"stream": s_lo, "span": p}),
            remote(sb.at[pl.ds(COLS, COLS)], rx.at[pl.ds(0, COLS)], base + 3, {"stream": s_hi, "span": p}),
        ]

    def send(sb, rx, faces, zs, rz, base, wait):
        table = split3(tab_s[...])
        sb[...] = dot(send_hot, table[0]) + (dot(send_hot, table[1]) + dot(send_hot, table[2]))
        zs[0] = faces[0, 0]
        zs[1] = faces[1, LAYERS - 1]
        if wait:
            pl.semaphore_wait(barrier, 4 + 2 * (GROUP - 1))
        copies = exchange(sb, rx, zs, rz, base)
        for copy in copies:
            copy.start()
        return copies, table

    copies1, table = send(sb1, rx1, zp_s, zs1, rz1, 0, True)

    for f in range(4):
        col = column(fs_ref[f : f + 1, :].astype(F32))
        oo_s[f * COLS : (f + 1) * COLS, :] = jnp.where(col == own_id, 1.0, 0.0).astype(BF16)
        or_s[f * COLS : (f + 1) * COLS, :] = jnp.where(col == rec_id, 1.0, 0.0).astype(BF16)
        if f >= 2:
            fy_s[f - 2] = jnp.broadcast_to(col, (COLS, 128))
    for a in range(3):
        for l in range(LAYERS):
            m_s[a, l * COLS : (l + 1) * COLS, :] = jnp.broadcast_to(
                column(met_ref[a, l : l + 1, :]), (COLS, 128)
            )

    def own_gather(table):
        hot = oo_s[...]
        g_s[...] = dot(hot, table[0]) + (dot(hot, table[1]) + dot(hot, table[2]))

    def far_gather(rx):
        hot = or_s[...]
        table = split3(rx[...])
        g_s[...] += dot(hot, table[0]) + (dot(hot, table[1]) + dot(hot, table[2]))

    own_gather(table)

    def second(l, rc, row):
        u = [u_s[v, pl.ds(row, CHUNK), :] for v in range(10)]
        v, pr, t, dv, dp, dt, s2, ds2 = primitive(u[:5], u[5:])
        for i, value in enumerate(v + [t] + dv + [dt]):
            w_s[pl.ds(pl.multiple_of(i * ROWS + row, CHUNK), CHUNK), :] = value
        for i, value in enumerate([pr, dp, s2, ds2]):
            c_s[i, pl.ds(row, CHUNK), :] = value

    each_chunk(second)
    high, low = split2(w_s[...])
    q_s[...] = dot(jnp.concatenate([high, low, high], axis=1), op_ref[...])

    for copy in copies1:
        copy.wait()
    far_gather(rx1)

    def face_masks(rc):
        masks = []
        for axis in range(3):
            lower, upper = digit[axis] == 0.0, digit[axis] == 4.0
            if axis == 1:
                lower = lower & (fy_s[0, pl.ds(rc, CHUNK), :] >= 0.0)
                upper = upper & (fy_s[1, pl.ds(rc, CHUNK), :] >= 0.0)
            masks.append((lower, upper))
        return masks

    def packed_pair(axis, pt, l, rc, faces, rz):
        if axis < 2:
            col = (pt * LAYERS + l) * 128
            return [
                g_s[pl.ds(f * COLS + rc, CHUNK), col : col + 128] for f in (2 * axis, 2 * axis + 1)
            ]
        below = rz[0, pt, pl.ds(rc, CHUNK), :] if l == 0 else faces[1, l - 1, pt, pl.ds(rc, CHUNK), :]
        above = (
            rz[1, pt, pl.ds(rc, CHUNK), :]
            if l == LAYERS - 1
            else faces[0, l + 1, pt, pl.ds(rc, CHUNK), :]
        )
        return [below, above]

    def unpack(pair, v, axis, masks, inside):
        stride = STRIDES[axis]
        upper = jnp.where(masks[axis][1], roll(pair[1], (4 - v) * stride), inside)
        return jnp.where(masks[axis][0], roll(pair[0], -v * stride), upper)

    def third(l, rc, row):
        masks = face_masks(rc)
        here = pl.ds(row, CHUNK)
        u = [u_s[v, here, :] for v in range(10)]
        inside = [-value if v % 5 in (1, 2, 3) else value for v, value in enumerate(u)]
        q = [[], []]
        for axis in range(3):
            out = []
            for pt in range(2):
                pair = packed_pair(axis, pt, l, rc, zp_s, rz1)
                for v in range(5):
                    out.append(unpack(pair, v, axis, masks, inside[pt * 5 + v]))
            for i, value in enumerate(out):
                o_s[axis, i, here, :] = value
            v, pr, t, dv, dp, dt, s2, ds2 = primitive(out[:5], out[5:])
            for i, value in enumerate(v + [pr, s2] + dv + [dp, ds2]):
                po_s[axis, i, here, :] = value
            factor = m_s[axis, here, :]
            for i, value in enumerate(v + [t] + dv + [dt]):
                volume = q_s[pl.ds(pl.multiple_of(i * ROWS + row, CHUNK), CHUNK), axis * 128 : axis * 128 + 128]
                q[i // 4].append(factor * (volume + sgn[axis] * value))
        w = [w_s[pl.ds(pl.multiple_of(i * ROWS + row, CHUNK), CHUNK), :] for i in range(8)]
        tau, dtau = [stress([q[pt][4 * a : 4 * a + 3] for a in range(3)]) for pt in range(2)]
        col = (l * 128, (LAYERS + l) * 128)
        for a in range(3):
            energy = COND * q[0][4 * a + 3]
            tangent = COND * q[1][4 * a + 3]
            for b in range(3):
                energy = energy + w[b] * tau[a][b]
                tangent = tangent + (w[4 + b] * tau[a][b] + w[b] * dtau[a][b])
            for pt, flux in enumerate((tau[a] + [energy], dtau[a] + [tangent])):
                for i, value in enumerate(flux):
                    v_s[a, pt * 4 + i, here, :] = value
                for up in range(2):
                    if a < 2:
                        tab_s[pl.ds((2 * a + up) * COLS + rc, CHUNK), col[pt] : col[pt] + 128] = pack(flux, a, up)
                    else:
                        zv_s[up, l, pt, pl.ds(rc, CHUNK), :] = pack(flux, a, up)

    each_chunk(third)
    copies2, table = send(sb2, rx2, zv_s, zs2, rz2, 4, False)

    own_gather(table)

    def fourth(l, rc, row):
        here = pl.ds(row, CHUNK)
        u = [u_s[v, here, :] for v in range(10)]
        w = [w_s[pl.ds(pl.multiple_of(i * ROWS + row, CHUNK), CHUNK), :] for i in range(8)]
        pr, dp, s2, ds2 = [c_s[i, here, :] for i in range(4)]
        total = [None] * 10
        for a in range(3):
            factor = m_s[a, here, :]
            flux, tangent = inviscid(u[:5], u[5:], w[:3], pr, w[4:7], dp, a)
            for pt, values in enumerate((flux, tangent)):
                for i, value in enumerate(values):
                    if i:
                        value = value - v_s[a, pt * 4 + i - 1, here, :]
                    at = pl.multiple_of((pt * 5 + i) * ROWS + row, CHUNK)
                    h_s[a, pl.ds(at, CHUNK), :] = factor * value
            out = [o_s[a, i, here, :] for i in range(10)]
            po = [po_s[a, i, here, :] for i in range(10)]
            flux, tangent = inviscid(out[:5], out[5:], po[:3], po[3], po[5:8], po[8], a)
            speed = jnp.sqrt(0.5 * (s2 + po[4]))
            dspeed = 0.25 * (ds2 + po[9]) / speed
            side = factor * sgn[a]
            drag = jnp.abs(side)
            for i in range(5):
                jump = out[i] - u[i]
                term = side * flux[i] - drag * (speed * jump)
                dterm = side * tangent[i] - drag * (dspeed * jump + speed * (out[5 + i] - u[5 + i]))
                total[i] = term if a == 0 else total[i] + term
                total[5 + i] = dterm if a == 0 else total[5 + i] + dterm
        for i in range(10):
            rs_s[i, here, :] = total[i]

    each_chunk(fourth)
    volume = None
    for a in range(3):
        high, low = split2(h_s[a])
        part = dot(jnp.concatenate([high, low, high], axis=1), op_ref[:, a * 128 : a * 128 + 128])
        volume = part if a == 0 else volume + part
    r_s[...] = volume

    for copy in copies2:
        copy.wait()
    far_gather(rx2)

    pt_s[...] = jnp.zeros((8, 128), F32)

    def fifth(l, rc, row):
        masks = face_masks(rc)
        here = pl.ds(row, CHUNK)
        total = [
            r_s[pl.ds(pl.multiple_of(i * ROWS + row, CHUNK), CHUNK), :] + rs_s[i, here, :]
            for i in range(10)
        ]
        for a in range(3):
            side = m_s[a, here, :] * sgn[a]
            for pt in range(2):
                pair = packed_pair(a, pt, l, rc, zv_s, rz2)
                for i in range(4):
                    value = unpack(pair, i, a, masks, v_s[a, pt * 4 + i, here, :])
                    total[pt * 5 + 1 + i] = total[pt * 5 + 1 + i] - side * value
        total = [jnp.where(node, value, 0.0) for value in total]
        du = [u_s[5 + i, here, :] for i in range(5)]
        sums = [None] * 4
        for i in range(5):
            terms = (
                du[i] * total[5 + i],
                du[i] * du[i],
                total[i] * total[i],
                total[5 + i] * total[5 + i],
            )
            sums = [term if i == 0 else old + term for old, term in zip(sums, terms)]
        for i in range(4):
            acc_s[i] += sums[i]
        for pt in range(2):
            fields = total[5 * pt : 5 * pt + 5]
            for t in range(5):
                value = roll(fields[t], -3 * t)
                if t < 4:
                    value = jnp.where(lane < 125 - 3 * t, value, roll(fields[t + 1], 125 - 3 * t))
                y_s[pt, here, 128 * t : 128 * t + 128] = value

    acc_s[...] = jnp.zeros((4, CHUNK, 128), F32)
    each_chunk(fifth)
    for i in range(4):
        pt_s[i : i + 1, :] = jnp.sum(acc_s[i], axis=0, keepdims=True)

    def stage(src, dst, mine, peer, send_sem, recv_sem):
        dst[mine] = src[...]

        def copy_to(k):
            target, j = peer(k)
            return pltpu.make_async_remote_copy(
                src_ref=src,
                dst_ref=dst.at[mine],
                send_sem=send_sem.at[k],
                recv_sem=recv_sem.at[k],
                device_id=target,
                device_id_type=MESH,
            )

        for k in range(1, GROUP):
            copy_to(k).start()
        return copy_to

    def collect(copy_to, dst):
        for k in range(1, GROUP):
            copy_to(k).wait()
        return jnp.sum(dst[...], axis=0)

    first_stage = stage(pt_s, ar_a, mine_a, peer_a, as_send, as_recv)
    for l in range(LAYERS):
        res_ref[:, l, :] = y_s[0, l * COLS : (l + 1) * COLS, 0:625]
    pb_s[...] = collect(first_stage, ar_a)
    second_stage = stage(pb_s, ar_b, mine_b, peer_b, bs_send, bs_recv)
    sums = collect(second_stage, ar_b)
    dp_sum, dd_sum, rr_sum, pp_sum = [
        jnp.sum(sums[i : i + 1, :], axis=1, keepdims=True) for i in range(4)
    ]
    count = 1.0 / float(n_s * n_p * ROWS * 625)
    coefficient = dp_sum * count
    beta = jnp.sqrt(
        (pp_sum - 2.0 * coefficient * dp_sum + coefficient * coefficient * dd_sum) * count
    )
    norm = jnp.sqrt(rr_sum * count)
    at = lax.broadcasted_iota(jnp.int32, (1, 128), 1)
    kry_ref[...] = jnp.where(at == 0, coefficient, jnp.where(at == 1, beta, norm))
    scale = 1.0 / beta
    for l in range(LAYERS):
        part = pl.ds(l * COLS, COLS)
        value = (y_s[1, part, :] - coefficient * x_s[1, part, :]) * scale
        bas_ref[:, l, :] = value[:, 0:625]


def local(state, direction, metric, face_source, send_rows):
    vmem = pl.BlockSpec(memory_space=pltpu.VMEM)
    shapes = [
        ((2, ROWS, 640), F32),
        ((10, ROWS, 128), F32),
        ((8 * ROWS, 128), F32),
        ((4, ROWS, 128), F32),
        ((3, ROWS, 128), F32),
        ((2, COLS, 128), F32),
        ((160, 160), BF16),
        ((160, 80), BF16),
        ((160, 512), F32),
        ((2, LAYERS, 2, COLS, 128), F32),
        ((2, LAYERS, 2, COLS, 128), F32),
        ((80, 512), F32),
        ((80, 512), F32),
        ((80, 512), F32),
        ((80, 512), F32),
        ((2, 2, COLS, 128), F32),
        ((2, 2, COLS, 128), F32),
        ((2, 2, COLS, 128), F32),
        ((2, 2, COLS, 128), F32),
        ((160, 512), F32),
        ((8 * ROWS, 384), F32),
        ((3, 10, ROWS, 128), F32),
        ((3, 10, ROWS, 128), F32),
        ((3, 8, ROWS, 128), F32),
        ((3, 10 * ROWS, 128), F32),
        ((10 * ROWS, 128), F32),
        ((10, ROWS, 128), F32),
        ((2, ROWS, 640), F32),
        ((4, CHUNK, 128), F32),
        ((8, 128), F32),
        ((8, 128), F32),
        ((GROUP, 8, 128), F32),
        ((GROUP, 8, 128), F32),
    ]
    res, bas, kry = pl.pallas_call(
        kernel,
        out_shape=(
            jax.ShapeDtypeStruct(state.shape, F32),
            jax.ShapeDtypeStruct(state.shape, F32),
            jax.ShapeDtypeStruct((1, 128), F32),
        ),
        in_specs=[vmem] * 7,
        out_specs=(vmem, vmem, vmem),
        scratch_shapes=[pltpu.VMEM(shape, dtype) for shape, dtype in shapes]
        + [pltpu.SemaphoreType.DMA((8,))] * 2
        + [pltpu.SemaphoreType.DMA((GROUP,))] * 4,
        compiler_params=pltpu.CompilerParams(
            collective_id=0, has_side_effects=True, vmem_limit_bytes=48 * 1024 * 1024
        ),
        name="hill",
    )(
        state,
        direction,
        jnp.transpose(metric, (2, 1, 0)),
        jnp.transpose(face_source),
        send_rows[0],
        jnp.asarray(operator_table()),
        jnp.asarray(lane_table()),
    )
    return res, bas, kry[0, :3]


def solution(mesh):
    in_specs = (
        P("stream", "span", None),
        P("stream", "span", None),
        P("stream", "span", None),
        P("stream", None),
        P("stream", None, None),
    )
    out_specs = (P("stream", "span", None), P("stream", "span", None), P())
    return jax.shard_map(local, mesh=mesh, in_specs=in_specs, out_specs=out_specs, check_vma=False)
```

profile of v0, /device:TPU:1, one launch (start us, length us, event | category | flops | bytes accessed | tf_op | source)
XLA Modules:
  0.0 46.5 jit_solution(9241286554977144360)
XLA Ops:
  0.6 0.0 copy-start.3
  0.6 0.0 copy-start.4
  0.7 0.7 %copy-done.3 = f32[8,128]{1,0:T(8,128)S(1)} copy-done((f32[8,128]{1,0:T(8,128)S(1)}, f32[8,128]{1,0:T(8,128)}, u32[]{:S(2)}) %copy-start.3) | copy-done | bytes 4120
  1.3 0.0 copy-done.4
  1.3 0.0 copy-start
  1.3 1.0 %copy-done = bf16[384,384]{1,0:T(8,128)(2,1)S(1)} copy-done((bf16[384,384]{1,0:T(8,128)(2,1)S(1)}, bf16[384,384]{1,0:T(8,128)(2,1)}, u32[]{:S(2)}) %copy-start) | copy-done | bytes 294936
  2.3 0.0 copy-start.1
  2.3 0.9 %copy-done.1 = f32[40,2,625]{2,1,0:T(2,128)S(1)} copy-done((f32[40,2,625]{2,1,0:T(2,128)S(1)}, f32[40,2,625]{2,1,0:T(2,128)}, u32[]{:S(2)}) %copy-start.1) | copy-done | bytes 200024
  3.2 0.0 copy-start.2
  3.2 0.9 %copy-done.2 = f32[40,2,625]{2,1,0:T(2,128)S(1)} copy-done((f32[40,2,625]{2,1,0:T(2,128)S(1)}, f32[40,2,625]{2,1,0:T(2,128)}, u32[]{:S(2)}) %copy-start.2) | copy-done | bytes 200024
  4.2 0.0 copy-start.5
  4.2 0.7 %copy-done.5 = s32[40,4]{0,1:T(4,128)S(1)} copy-done((s32[40,4]{0,1:T(4,128)S(1)}, s32[40,4]{0,1:T(4,128)}, u32[]{:S(2)}) %copy-start.5) | copy-done | bytes 664
  4.8 0.0 copy-start.6
  4.8 0.7 %copy-done.6 = s32[1,2,33]{2,1,0:T(2,128)S(1)} copy-done((s32[1,2,33]{2,1,0:T(2,128)S(1)}, s32[1,2,33]{2,1,0:T(2,128)}, u32[]{:S(2)}) %copy-start.6) | copy-done | bytes 288
  5.5 39.1 %hill.1 = (f32[40,2,625]{2,1,0:T(2,128)S(1)}, f32[40,2,625]{2,1,0:T(2,128)S(1)}, f32[1,128]{1,0:T(1,128)S(1)}) custom-call(f32[40,2,625]{2,1,0:T(2,128)S(1)} %copy-done.1, f32[40,2,625]{2,1,0:T(2,128)S(1)} %copy-done.2, f32[3,2,40]{2,1,0:T(2,128)S(1)} %bitcast.5, s32[4,40]{1,0:T(4,128)S(1)} %bitcast.6, s32[2,33]{1,0:T(2,128)S(1)} %bitcast.7, ...), custom_call_target="tpu_custom_call" | custom-call | tf_op jit(solution)/shard_map/hill/pallas_call | solution.py:619
  44.6 0.5 %slice_bitcast_fusion = f32[3]{0:T(128)} fusion(f32[1,128]{1,0:T(1,128)S(1)} %get-tuple-element.8), kind=kLoop, calls=%fused_computation | loop fusion | bytes 24 | tf_op jit(solution)/shard_map/squeeze | solution.py:644
  45.2 0.7 %copy.12 = f32[40,2,625]{2,1,0:T(2,128)} copy(f32[40,2,625]{2,1,0:T(2,128)S(1)} %get-tuple-element.12) | data formatting | bytes 400000
  45.8 0.7 %copy.13 = f32[40,2,625]{2,1,0:T(2,128)} copy(f32[40,2,625]{2,1,0:T(2,128)S(1)} %get-tuple-element.13) | data formatting | bytes 400000
Async XLA Ops:
  0.6 0.7 %copy-start.3 = (f32[8,128]{1,0:T(8,128)S(1)}, f32[8,128]{1,0:T(8,128)}, u32[]{:S(2)}) copy-start(f32[8,128]{1,0:T(8,128)} %constant.5.clone.lane_ref) | copy-start | bytes 12292
  0.6 0.7 %copy-start.4 = (f32[40,2,3]{0,1,2:T(2,128)S(1)}, f32[40,2,3]{0,1,2:T(2,128)}, u32[]{:S(2)}) copy-start(f32[40,2,3]{0,1,2:T(2,128)} %param.9) | copy-start | bytes 2884
  1.3 1.0 %copy-start = (bf16[384,384]{1,0:T(8,128)(2,1)S(1)}, bf16[384,384]{1,0:T(8,128)(2,1)}, u32[]{:S(2)}) copy-start(bf16[384,384]{1,0:T(8,128)(2,1)} %constant.4.clone.op_ref) | copy-start | bytes 884740
  2.3 0.9 %copy-start.1 = (f32[40,2,625]{2,1,0:T(2,128)S(1)}, f32[40,2,625]{2,1,0:T(2,128)}, u32[]{:S(2)}) copy-start(f32[40,2,625]{2,1,0:T(2,128)} %state_ref.1) | copy-start | bytes 600004
  3.2 0.9 %copy-start.2 = (f32[40,2,625]{2,1,0:T(2,128)S(1)}, f32[40,2,625]{2,1,0:T(2,128)}, u32[]{:S(2)}) copy-start(f32[40,2,625]{2,1,0:T(2,128)} %dir_ref.1) | copy-start | bytes 600004
  4.2 0.7 %copy-start.5 = (s32[40,4]{0,1:T(4,128)S(1)}, s32[40,4]{0,1:T(4,128)}, u32[]{:S(2)}) copy-start(s32[40,4]{0,1:T(4,128)} %param.10) | copy-start | bytes 1924
  4.8 0.7 %copy-start.6 = (s32[1,2,33]{2,1,0:T(2,128)S(1)}, s32[1,2,33]{2,1,0:T(2,128)}, u32[]{:S(2)}) copy-start(s32[1,2,33]{2,1,0:T(2,128)} %param.11) | copy-start | bytes 796
where the time goes:
time: 46.8 us; the launch traced here: 46.5 us
  Pallas kernels  39.1 us (84%)
  local copies, waits for them, and re-layouts  6.74 us (14%)
  between operations  0.66 us (1%)
    pallas_call x1, Pallas kernels, local(): pl.pallas_call(kernel, out_shape=(jax.ShapeDtypeStruct(state.shape, F32),...  39.1 us
    unnamed x16, local copies, waits for them, and re-layouts  6.23 us

commit v1 on v0

v1 whole, which is shorter than its diff:
```python
import math

import jax
import jax.numpy as jnp
import numpy as np
from jax import lax
from jax.experimental import pallas as pl
from jax.experimental.pallas import tpu as pltpu
from jax.sharding import PartitionSpec as P

MESH = pl.DeviceIdType.MESH
F32 = jnp.float32
BF16 = jnp.bfloat16

GAMMA = 1.4
VISC = 0.01
COND = VISC * GAMMA / ((GAMMA - 1.0) * 0.72)

COLS = 40
LAYERS = 2
ROWS = COLS * LAYERS
SLOTS = 33
SENT = 40
CHUNK = 8
STRIDES = (25, 5, 1)
N_X, N_Z, N_SPAN = 4, 8, 4
PLANE = 2 * N_X * N_SPAN


def diff_table():
    spread = math.sqrt(3.0 / 7.0)
    points = np.array([-1.0, -spread, 0.0, spread, 1.0])
    weights = np.array(
        [
            np.prod([points[row_at] - points[other] for other in range(5) if other != row_at])
            for row_at in range(5)
        ]
    )
    matrix = np.zeros((5, 5))
    for row_at in range(5):
        for col_at in range(5):
            if row_at != col_at:
                matrix[row_at, col_at] = weights[row_at] / (
                    weights[col_at] * (points[row_at] - points[col_at])
                )
        matrix[row_at, row_at] = np.sum(
            [1.0 / (points[row_at] - points[other]) for other in range(5) if other != row_at]
        )
    return matrix


def operator_table():
    line = diff_table()
    line[0, 0] += 5.0
    line[4, 4] -= 5.0
    eye = np.eye(5)
    full = np.zeros((128, 384), np.float32)
    for axis in range(3):
        parts = [eye, eye, eye]
        parts[axis] = line
        volume = np.kron(np.kron(parts[0], parts[1]), parts[2])
        full[:125, axis * 128 : axis * 128 + 125] = volume.T
    high = full.astype(jnp.bfloat16)
    low = (full - high.astype(np.float32)).astype(jnp.bfloat16)
    return np.concatenate([high, high, low], axis=0)


def lane_table():
    table = np.zeros((16, 128), np.float32)
    lanes = np.arange(125)
    for axis, stride in enumerate(STRIDES):
        digit = (lanes // stride) % 5
        table[axis] = 9.0
        table[axis, :125] = digit
        table[3 + axis, :125] = 5.0 * (digit == 4) - 5.0 * (digit == 0)
        table[6 + axis] = 9.0
        for var in range(5):
            table[6 + axis, (lanes[digit == 4] + var * stride) % 128] = var
    return table


def roll(value, shift):
    shift %= 128
    return value if shift == 0 else pltpu.roll(value, shift, 1)


def split2(value):
    high = value.astype(BF16)
    return high, (value - high.astype(F32)).astype(BF16)


def split3(value):
    high = value.astype(BF16)
    rest = value - high.astype(F32)
    mid = rest.astype(BF16)
    return high, mid, (rest - mid.astype(F32)).astype(BF16)


def dot(a, b):
    return lax.dot_general(a, b, (((1,), (0,)), ((), ())), preferred_element_type=F32)


def primitive(u, du):
    r = 1.0 / u[0]
    v = [u[1 + i] * r for i in range(3)]
    dv = [(du[1 + i] - v[i] * du[0]) * r for i in range(3)]
    vm = u[1] * v[0] + u[2] * v[1] + u[3] * v[2]
    p = (GAMMA - 1.0) * (u[4] - 0.5 * vm)
    vdm = v[0] * du[1] + v[1] * du[2] + v[2] * du[3]
    vv = v[0] * v[0] + v[1] * v[1] + v[2] * v[2]
    dp = (GAMMA - 1.0) * (du[4] - vdm + 0.5 * vv * du[0])
    t = p * r
    dt = (dp - t * du[0]) * r
    s2 = vv + GAMMA * t
    ds2 = 2.0 * (v[0] * dv[0] + v[1] * dv[1] + v[2] * dv[2]) + GAMMA * dt
    return v, p, t, dv, dp, dt, s2, ds2


def inviscid(u, du, v, p, dv, dp, axis):
    flux = [u[1 + axis]]
    tangent = [du[1 + axis]]
    for i in range(3):
        f = u[1 + i] * v[axis]
        df = du[1 + i] * v[axis] + u[1 + i] * dv[axis]
        if i == axis:
            f = f + p
            df = df + dp
        flux.append(f)
        tangent.append(df)
    flux.append((u[4] + p) * v[axis])
    tangent.append((du[4] + dp) * v[axis] + (u[4] + p) * dv[axis])
    return flux, tangent


def stress(q):
    third = (2.0 / 3.0) * (q[0][0] + q[1][1] + q[2][2])
    tau = [[None] * 3 for _ in range(3)]
    for a in range(3):
        tau[a][a] = VISC * (2.0 * q[a][a] - third)
        for b in range(a + 1, 3):
            tau[a][b] = tau[b][a] = VISC * (q[a][b] + q[b][a])
    return tau


def kernel(
    state_in,
    dir_in,
    met_in,
    fs_in,
    sr_in,
    op_in,
    lane_in,
    res_ref,
    bas_ref,
    kry_ref,
    state_ref,
    dir_ref,
    met_ref,
    fs_ref,
    sr_ref,
    op_ref,
    lane_ref,
    x_s,
    u_s,
    w_s,
    c_s,
    m_s,
    fy_s,
    oo_s,
    or_s,
    so_s,
    tab_s,
    zp_s,
    zv_s,
    sb1,
    sb2,
    rx1,
    rx2,
    rz1,
    rz2,
    g_s,
    q_s,
    o_s,
    po_s,
    v_s,
    h_s,
    r_s,
    rs_s,
    y_s,
    x_out,
    acc_s,
    pt_s,
    pb_s,
    ar_a,
    ar_b,
    xs_send,
    xs_recv,
    sum_sem,
    in_sem,
):
    loads = [
        pltpu.make_async_copy(src, dst, in_sem.at[i])
        for i, (src, dst) in enumerate(
            (
                (state_in, state_ref),
                (dir_in, dir_ref),
                (lane_in, lane_ref),
                (sr_in, sr_ref),
                (fs_in, fs_ref),
                (met_in, met_ref),
                (op_in, op_ref),
            )
        )
    ]
    for load in loads:
        load.start()

    s = lax.axis_index("stream")
    p = lax.axis_index("span")
    n_s = 2 * N_X * N_Z
    s_lo, s_hi = lax.rem(s + n_s - 1, n_s), lax.rem(s + 1, n_s)
    p_lo, p_hi = lax.rem(p + N_SPAN - 1, N_SPAN), lax.rem(p + 1, N_SPAN)
    core = lax.rem(p, 2)
    x_at, z_at, y_hi, y_lo = s // (2 * N_Z), lax.rem(s // 2, N_Z), lax.rem(s, 2), p // 2
    chip = 4 * x_at + 2 * y_hi + y_lo
    mine = 2 * chip + core

    def plane_peer(j):
        return {
            "stream": (j // 8) * (2 * N_Z) + 2 * z_at + lax.rem(j // 4, 2),
            "span": lax.rem(j, 4),
        }

    def column_peer(z, c):
        return {"stream": x_at * (2 * N_Z) + 2 * z + y_hi, "span": 2 * y_lo + c}

    barrier = pltpu.get_barrier_semaphore()

    def greet(target):
        pl.semaphore_signal(barrier, inc=1, device_id=target, device_id_type=MESH)

    greet({"stream": s_lo, "span": p})
    greet({"stream": s_hi, "span": p})
    greet({"stream": s, "span": p_lo})
    greet({"stream": s, "span": p_hi})

    for k in range(1, N_Z):
        greet(column_peer(lax.rem(z_at + k, N_Z), 1))

    @pl.when(core == 1)
    def _():
        for k in range(1, PLANE):
            greet(plane_peer(lax.rem(mine + k, PLANE)))

    @pl.when(core == 0)
    def _():
        greet(column_peer(z_at, 1))

    for load in loads[:3]:
        load.wait()
    lane = lax.broadcasted_iota(jnp.int32, (CHUNK, 128), 1)
    rows = [jnp.broadcast_to(lane_ref[a : a + 1, :], (CHUNK, 128)) for a in range(9)]
    digit, sgn, over = rows[:3], rows[3:6], rows[6:]
    node = lane < 125

    for l in range(LAYERS):
        x_s[0, l * COLS : (l + 1) * COLS, 0:625] = state_ref[:, l, :]
        x_s[1, l * COLS : (l + 1) * COLS, 0:625] = dir_ref[:, l, :]

    def pack(fields, axis):
        stride = STRIDES[axis]
        lower = upper = fields[0]
        for v, field in enumerate(fields):
            if v:
                moved = roll(field, v * stride)
                lower = jnp.where(digit[axis] == float(v), moved, lower)
                upper = jnp.where(over[axis] == float(v), moved, upper)
        return roll(lower, 4 * stride), roll(upper, -4 * stride)

    def pack_axis(fields, axis, pt, l, rc, faces):
        for up, value in enumerate(pack(fields, axis)):
            if axis < 2:
                at = (2 * axis + up) * COLS + rc
                tab_s[l, pl.ds(at, CHUNK), pt * 128 : pt * 128 + 128] = value
            else:
                faces[up, l, pt, pl.ds(rc, CHUNK), :] = value

    def layer_loop(body, l):
        def step(i, carry):
            rc = pl.multiple_of(i * CHUNK, CHUNK)
            body(l, rc, pl.multiple_of(l * COLS + rc, CHUNK))
            return carry

        lax.fori_loop(0, COLS // CHUNK, step, 0, unroll=COLS // CHUNK)

    def first(l, rc, row):
        for pt in range(2):
            tiles = [x_s[pt, pl.ds(row, CHUNK), 128 * t : 128 * t + 128] for t in range(5)]
            fields = []
            for v in range(5):
                value = roll(tiles[v], 3 * v)
                if v:
                    value = jnp.where(lane < 3 * v, roll(tiles[v - 1], 3 * v), value)
                idle = 1.0 if pt == 0 and v in (0, 4) else 0.0
                value = jnp.where(node, value, idle)
                u_s[pt * 5 + v, pl.ds(row, CHUNK), :] = value
                fields.append(value)
            for axis in range(3):
                pack_axis(fields, axis, pt, l, rc, zp_s)

    def remote(src, dst, sem, target):
        return pltpu.make_async_remote_copy(
            src_ref=src,
            dst_ref=dst,
            send_sem=xs_send.at[sem],
            recv_sem=xs_recv.at[sem],
            device_id=target,
            device_id_type=MESH,
        )

    def z_copies(faces, rz, base):
        return [
            remote(faces.at[0, 0], rz.at[1], base, {"stream": s, "span": p_lo}),
            remote(faces.at[1, LAYERS - 1], rz.at[0], base + 1, {"stream": s, "span": p_hi}),
        ]

    def xy_copies(sb, rx, l, base):
        lower, upper = pl.ds(0, SENT), pl.ds(COLS, SENT)
        return [
            remote(sb.at[l, lower], rx.at[l, upper], base + 2 + 2 * l, {"stream": s_lo, "span": p}),
            remote(sb.at[l, upper], rx.at[l, lower], base + 3 + 2 * l, {"stream": s_hi, "span": p}),
        ]

    def start(copies):
        for copy in copies:
            copy.start()

    def wait(copies):
        for copy in copies:
            copy.wait()

    def gather(hot, table):
        parts = split3(table)
        return dot(hot, parts[0]) + (dot(hot, parts[1]) + dot(hot, parts[2]))

    def fill(sb, l):
        sb[l] = gather(so_s[...], tab_s[l])

    with jax.named_scope("first0"):
        layer_loop(first, 0)

    for load in loads[3:]:
        load.wait()
    eye = lax.broadcasted_iota(jnp.int32, (COLS, COLS), 0) == lax.broadcasted_iota(
        jnp.int32, (COLS, COLS), 1
    )

    def column(row):
        return jnp.sum(
            jnp.where(eye, jnp.broadcast_to(row, (COLS, COLS)), 0.0), axis=1, keepdims=True
        )

    k_own = lax.broadcasted_iota(jnp.int32, (COLS, 160), 1)
    g_own = (
        jnp.where(k_own >= 40, 159, 0)
        + jnp.where(k_own >= 80, 159, 0)
        + jnp.where(k_own >= 120, 159, 0)
    )
    own_id = (4 * k_own - g_own).astype(F32)
    k_rec = lax.broadcasted_iota(jnp.int32, (COLS, 80), 1)
    rec_id = jnp.where(
        k_rec < SLOTS,
        k_rec + 160,
        jnp.where((k_rec >= COLS) & (k_rec < COLS + SLOTS), k_rec + 153, -5),
    ).astype(F32)
    slot = lax.broadcasted_iota(jnp.int32, (COLS, SLOTS), 0) == lax.broadcasted_iota(
        jnp.int32, (COLS, SLOTS), 1
    )
    for side in range(2):
        ids = sr_ref[side : side + 1, :].astype(F32)
        col = jnp.sum(
            jnp.where(slot, jnp.broadcast_to(ids, (COLS, SLOTS)), 0.0), axis=1, keepdims=True
        )
        so_s[side * COLS : (side + 1) * COLS, :] = jnp.where(col == own_id, 1.0, 0.0).astype(BF16)

    round1 = [xy_copies(sb1, rx1, l, 0) for l in range(LAYERS)]
    round1_z = z_copies(zp_s, rz1, 0)
    round2 = [xy_copies(sb2, rx2, l, 6) for l in range(LAYERS)]
    round2_z = z_copies(zv_s, rz2, 6)

    fill(sb1, 0)
    with jax.named_scope("barrier"):
        pl.semaphore_wait(barrier, 4 + 16 + 14 * core)
    start(round1[0])
    with jax.named_scope("first1"):
        layer_loop(first, 1)
        start(round1_z)
        fill(sb1, 1)
        start(round1[1])

    for f in range(4):
        col = column(fs_ref[f : f + 1, :].astype(F32))
        oo_s[f * COLS : (f + 1) * COLS, :] = jnp.where(col == own_id, 1.0, 0.0).astype(BF16)
        or_s[f * COLS : (f + 1) * COLS, :] = jnp.where(col == rec_id, 1.0, 0.0).astype(BF16)
        if f >= 2:
            fy_s[f - 2] = jnp.broadcast_to(col, (COLS, 128))
    for a in range(3):
        for l in range(LAYERS):
            m_s[a, l * COLS : (l + 1) * COLS, :] = jnp.broadcast_to(
                column(met_ref[a, l : l + 1, :]), (COLS, 128)
            )

    def own_gather(l):
        g_s[l] = gather(oo_s[...], tab_s[l])

    def far_gather(rx, l):
        table = rx[l]
        if SENT < COLS:
            at = lax.broadcasted_iota(jnp.int32, (2 * COLS, 256), 0)
            used = (at < SLOTS) | ((at >= COLS) & (at < COLS + SLOTS))
            table = jnp.where(used, table, 0.0)
        g_s[l] += gather(or_s[...], table)

    def second(l, rc, row):
        u = [u_s[v, pl.ds(row, CHUNK), :] for v in range(10)]
        v, pr, t, dv, dp, dt, s2, ds2 = primitive(u[:5], u[5:])
        for i, value in enumerate(v + [t] + dv + [dt]):
            w_s[pl.ds(pl.multiple_of(i * ROWS + row, CHUNK), CHUNK), :] = value
        for i, value in enumerate([pr, dp, s2, ds2]):
            c_s[i, pl.ds(row, CHUNK), :] = value

    for l in range(LAYERS):
        layer_loop(second, l)
    high, low = split2(w_s[...])
    q_s[...] = dot(jnp.concatenate([high, low, high], axis=1), op_ref[...])
    for l in range(LAYERS):
        own_gather(l)

    def face_masks(rc):
        masks = []
        for axis in range(3):
            lower, upper = digit[axis] == 0.0, digit[axis] == 4.0
            if axis == 1:
                lower = lower & (fy_s[0, pl.ds(rc, CHUNK), :] >= 0.0)
                upper = upper & (fy_s[1, pl.ds(rc, CHUNK), :] >= 0.0)
            masks.append(lower | upper)
        return masks

    def packed_pair(axis, pt, l, rc, faces, rz):
        here = pl.ds(rc, CHUNK)
        if axis < 2:
            return [
                g_s[l, pl.ds(f * COLS + rc, CHUNK), pt * 128 : pt * 128 + 128]
                for f in (2 * axis, 2 * axis + 1)
            ]
        below = rz[0, pt, here, :] if l == 0 else faces[1, l - 1, pt, here, :]
        above = rz[1, pt, here, :] if l == LAYERS - 1 else faces[0, l + 1, pt, here, :]
        return [below, above]

    def unpack(pair, v, axis, masks, inside):
        mixed = jnp.where(digit[axis] == float(v), pair[0], pair[1])
        return jnp.where(masks[axis], roll(mixed, -v * STRIDES[axis]), inside)

    def third(l, rc, row):
        masks = face_masks(rc)
        here = pl.ds(row, CHUNK)
        u = [u_s[v, here, :] for v in range(10)]
        inside = [-value if v % 5 in (1, 2, 3) else value for v, value in enumerate(u)]
        q = [[], []]
        for axis in range(3):
            out = []
            for pt in range(2):
                pair = packed_pair(axis, pt, l, rc, zp_s, rz1)
                for v in range(5):
                    out.append(unpack(pair, v, axis, masks, inside[pt * 5 + v]))
            for i, value in enumerate(out):
                o_s[axis, i, here, :] = value
            v, pr, t, dv, dp, dt, s2, ds2 = primitive(out[:5], out[5:])
            for i, value in enumerate(v + [pr, s2] + dv + [dp, ds2]):
                po_s[axis, i, here, :] = value
            factor = m_s[axis, here, :]
            for i, value in enumerate(v + [t] + dv + [dt]):
                at = pl.multiple_of(i * ROWS + row, CHUNK)
                volume = q_s[pl.ds(at, CHUNK), axis * 128 : axis * 128 + 128]
                q[i // 4].append(factor * (volume + sgn[axis] * value))
        w = [w_s[pl.ds(pl.multiple_of(i * ROWS + row, CHUNK), CHUNK), :] for i in range(8)]
        tau, dtau = [stress([q[pt][4 * a : 4 * a + 3] for a in range(3)]) for pt in range(2)]
        for a in range(3):
            energy = COND * q[0][4 * a + 3]
            tangent = COND * q[1][4 * a + 3]
            for b in range(3):
                energy = energy + w[b] * tau[a][b]
                tangent = tangent + (w[4 + b] * tau[a][b] + w[b] * dtau[a][b])
            for pt, flux in enumerate((tau[a] + [energy], dtau[a] + [tangent])):
                for i, value in enumerate(flux):
                    v_s[a, pt * 4 + i, here, :] = value
                pack_axis(flux, a, pt, l, rc, zv_s)

    with jax.named_scope("wait1z"):
        wait(round1_z)
    for l in range(LAYERS):
        with jax.named_scope("wait1"):
            wait(round1[l])
        with jax.named_scope("third"):
            far_gather(rx1, l)
            layer_loop(third, l)
            start(round2_z[l : l + 1])
            fill(sb2, l)
            start(round2[l])

    def fourth(l, rc, row):
        here = pl.ds(row, CHUNK)
        u = [u_s[v, here, :] for v in range(10)]
        w = [w_s[pl.ds(pl.multiple_of(i * ROWS + row, CHUNK), CHUNK), :] for i in range(8)]
        pr, dp, s2, ds2 = [c_s[i, here, :] for i in range(4)]
        total = [None] * 10
        for a in range(3):
            factor = m_s[a, here, :]
            flux, tangent = inviscid(u[:5], u[5:], w[:3], pr, w[4:7], dp, a)
            for pt, values in enumerate((flux, tangent)):
                for i, value in enumerate(values):
                    if i:
                        value = value - v_s[a, pt * 4 + i - 1, here, :]
                    at = pl.multiple_of((pt * 5 + i) * ROWS + row, CHUNK)
                    h_s[a, pl.ds(at, CHUNK), :] = factor * value
            out = [o_s[a, i, here, :] for i in range(10)]
            po = [po_s[a, i, here, :] for i in range(10)]
            flux, tangent = inviscid(out[:5], out[5:], po[:3], po[3], po[5:8], po[8], a)
            speed = jnp.sqrt(0.5 * (s2 + po[4]))
            dspeed = 0.25 * (ds2 + po[9]) / speed
            side = factor * sgn[a]
            drag = jnp.abs(side)
            for i in range(5):
                jump = out[i] - u[i]
                term = side * flux[i] - drag * (speed * jump)
                dterm = side * tangent[i] - drag * (dspeed * jump + speed * (out[5 + i] - u[5 + i]))
                total[i] = term if a == 0 else total[i] + term
                total[5 + i] = dterm if a == 0 else total[5 + i] + dterm
        for i in range(10):
            rs_s[i, here, :] = total[i]

    with jax.named_scope("fourth"):
        for l in range(LAYERS):
            own_gather(l)
            layer_loop(fourth, l)
    with jax.named_scope("resmm"):
        volume = None
        for a in range(3):
            high, low = split2(h_s[a])
            part = dot(jnp.concatenate([high, low, high], axis=1), op_ref[:, a * 128 : a * 128 + 128])
            volume = part if a == 0 else volume + part
        r_s[...] = volume
        acc_s[...] = jnp.zeros((4, CHUNK, 128), F32)

    def fifth(l, rc, row):
        masks = face_masks(rc)
        here = pl.ds(row, CHUNK)
        total = [
            r_s[pl.ds(pl.multiple_of(i * ROWS + row, CHUNK), CHUNK), :] + rs_s[i, here, :]
            for i in range(10)
        ]
        for a in range(3):
            side = m_s[a, here, :] * sgn[a]
            for pt in range(2):
                pair = packed_pair(a, pt, l, rc, zv_s, rz2)
                for i in range(4):
                    value = unpack(pair, i, a, masks, v_s[a, pt * 4 + i, here, :])
                    total[pt * 5 + 1 + i] = total[pt * 5 + 1 + i] - side * value
        total = [jnp.where(node, value, 0.0) for value in total]
        du = [u_s[5 + i, here, :] for i in range(5)]
        sums = [None] * 4
        for i in range(5):
            terms = (
                du[i] * total[5 + i],
                du[i] * du[i],
                total[i] * total[i],
                total[5 + i] * total[5 + i],
            )
            sums = [term if i == 0 else old + term for old, term in zip(sums, terms)]
        for i in range(4):
            acc_s[i] += sums[i]
        for i in range(10):
            y_s[i, here, :] = total[i]

    with jax.named_scope("wait2z"):
        wait(round2_z)
    for l in range(LAYERS):
        with jax.named_scope("wait2"):
            wait(round2[l])
        with jax.named_scope("fifth"):
            far_gather(rx2, l)
            layer_loop(fifth, l)

    at = lax.broadcasted_iota(jnp.int32, (1, 128), 1)
    own = [jnp.sum(acc_s[i], axis=(0, 1), keepdims=True) for i in range(4)]
    own = jnp.where(at == 0, own[0], jnp.where(at == 1, own[1], jnp.where(at == 2, own[2], own[3])))
    pt_s[...] = own

    def to_plane(k):
        return pltpu.make_async_remote_copy(
            src_ref=pt_s,
            dst_ref=ar_a.at[mine],
            send_sem=sum_sem.at[0],
            recv_sem=sum_sem.at[1],
            device_id=plane_peer(2 * lax.rem(chip + k, PLANE // 2) + 1),
            device_id_type=MESH,
        )

    def to_column(k, c):
        return pltpu.make_async_remote_copy(
            src_ref=pb_s,
            dst_ref=ar_b.at[z_at],
            send_sem=sum_sem.at[2],
            recv_sem=sum_sem.at[3],
            device_id=column_peer(lax.rem(z_at + k, N_Z), c),
            device_id_type=MESH,
        )

    def drain(buffer, count, sem):
        part = buffer.at[pl.ds(0, count)]
        pltpu.make_async_copy(part, part, sum_sem.at[sem]).wait()

    for k in range(1, PLANE // 2):
        to_plane(k).start()

    @pl.when(core == 0)
    def _():
        to_plane(0).start()

    @pl.when(core == 1)
    def _():
        ar_a[mine] = own

    def tile(fields, t):
        value = roll(fields[t], -3 * t)
        if t < 4:
            value = jnp.where(lane < 125 - 3 * t, value, roll(fields[t + 1], 125 - 3 * t))
        return value

    def sixth(l, rc, row):
        here = pl.ds(row, CHUNK)
        fields = [y_s[i, here, :] for i in range(10)]
        for pt in range(2):
            for t in range(5):
                x_out[pt, here, 128 * t : 128 * t + 128] = tile(fields[5 * pt : 5 * pt + 5], t)

    with jax.named_scope("sixth"):
        for l in range(LAYERS):
            layer_loop(sixth, l)
        for l in range(LAYERS):
            res_ref[:, l, :] = x_out[0, l * COLS : (l + 1) * COLS, 0:625]

    with jax.named_scope("sums"):

        @pl.when(core == 1)
        def _():
            drain(ar_a, PLANE - 1, 1)
            total = jnp.sum(ar_a[...], axis=0)
            pb_s[...] = total
            for k in range(1, N_Z):
                to_column(k, 1).start()
                to_column(k, 0).start()
            to_column(0, 0).start()
            ar_b[z_at] = total
            drain(ar_b, N_Z - 1, 3)

        @pl.when(core == 0)
        def _():
            drain(ar_b, N_Z, 3)

    sums = jnp.sum(ar_b[...], axis=0)
    dp_sum, dd_sum, rr_sum, pp_sum = [
        jnp.sum(jnp.where(at == i, sums, 0.0), axis=1, keepdims=True) for i in range(4)
    ]
    count = 1.0 / float(n_s * N_SPAN * ROWS * 625)
    coefficient = dp_sum * count
    beta = jnp.sqrt(
        (pp_sum - 2.0 * coefficient * dp_sum + coefficient * coefficient * dd_sum) * count
    )
    norm = jnp.sqrt(rr_sum * count)
    kry_ref[...] = jnp.where(at == 0, coefficient, jnp.where(at == 1, beta, norm))
    scale = 1.0 / beta
    for l in range(LAYERS):
        part = pl.ds(l * COLS, COLS)
        value = (x_out[1, part, :] - coefficient * x_s[1, part, :]) * scale
        bas_ref[:, l, :] = value[:, 0:625]

    @pl.when(core == 0)
    def _():
        drain(ar_a, PLANE // 2, 0)

    @pl.when(core == 1)
    def _():
        drain(ar_a, PLANE // 2 - 1, 0)
        drain(ar_a, 2 * N_Z - 1, 2)


def tail(res_in, bas_in, kry_in, res_out, bas_out, kry_out, sem):
    copies = [
        pltpu.make_async_copy(res_in, res_out, sem.at[0]),
        pltpu.make_async_copy(bas_in, bas_out, sem.at[1]),
    ]
    for copy in copies:
        copy.start()
    for i in range(3):
        kry_out[i] = jnp.sum(kry_in[0:1, i : i + 1])
    for copy in copies:
        copy.wait()


def local(state, direction, metric, face_source, send_rows):
    vmem = pl.BlockSpec(memory_space=pltpu.VMEM)
    hbm = pl.BlockSpec(memory_space=pltpu.HBM)
    shapes = [
        (state.shape, F32),
        (state.shape, F32),
        ((3, LAYERS, COLS), F32),
        ((4, COLS), jnp.int32),
        ((2, SLOTS), jnp.int32),
        ((384, 384), BF16),
        ((16, 128), F32),
        ((2, ROWS, 640), F32),
        ((10, ROWS, 128), F32),
        ((8 * ROWS, 128), F32),
        ((4, ROWS, 128), F32),
        ((3, ROWS, 128), F32),
        ((2, COLS, 128), F32),
        ((160, 160), BF16),
        ((160, 80), BF16),
        ((80, 160), BF16),
        ((LAYERS, 160, 256), F32),
        ((2, LAYERS, 2, COLS, 128), F32),
        ((2, LAYERS, 2, COLS, 128), F32),
        ((LAYERS, 80, 256), F32),
        ((LAYERS, 80, 256), F32),
        ((LAYERS, 80, 256), F32),
        ((LAYERS, 80, 256), F32),
        ((2, 2, COLS, 128), F32),
        ((2, 2, COLS, 128), F32),
        ((LAYERS, 160, 256), F32),
        ((8 * ROWS, 384), F32),
        ((3, 10, ROWS, 128), F32),
        ((3, 10, ROWS, 128), F32),
        ((3, 8, ROWS, 128), F32),
        ((3, 10 * ROWS, 128), F32),
        ((10 * ROWS, 128), F32),
        ((10, ROWS, 128), F32),
        ((10, ROWS, 128), F32),
        ((2, ROWS, 640), F32),
        ((4, CHUNK, 128), F32),
        ((1, 128), F32),
        ((1, 128), F32),
        ((PLANE, 1, 128), F32),
        ((N_Z, 1, 128), F32),
    ]
    res, bas, kry = pl.pallas_call(
        kernel,
        out_shape=(
            pltpu.VMEM(state.shape, F32),
            pltpu.VMEM(state.shape, F32),
            pltpu.VMEM((1, 128), F32),
        ),
        in_specs=[hbm] * 7,
        out_specs=(vmem, vmem, vmem),
        scratch_shapes=[pltpu.VMEM(shape, dtype) for shape, dtype in shapes]
        + [pltpu.SemaphoreType.DMA((n,)) for n in (12, 12, 4, 7)],
        compiler_params=pltpu.CompilerParams(
            collective_id=0, has_side_effects=True, vmem_limit_bytes=48 * 1024 * 1024
        ),
        name="hill",
    )(
        *[
            pltpu.with_memory_space_constraint(value, pltpu.HBM)
            for value in (
                state,
                direction,
                jnp.transpose(metric, (2, 1, 0)),
                jnp.transpose(face_source),
                send_rows[0],
                jnp.asarray(operator_table()),
                jnp.asarray(lane_table()),
            )
        ]
    )
    return pl.pallas_call(
        tail,
        out_shape=(
            pltpu.HBM(state.shape, F32),
            pltpu.HBM(state.shape, F32),
            jax.ShapeDtypeStruct((3,), F32),
        ),
        in_specs=[vmem] * 3,
        out_specs=(hbm, hbm, pl.BlockSpec(memory_space=pltpu.SMEM)),
        scratch_shapes=[pltpu.SemaphoreType.DMA((2,))],
        compiler_params=pltpu.CompilerParams(vmem_limit_bytes=1024 * 1024),
        name="tail",
    )(res, bas, kry)


def solution(mesh):
    in_specs = (
        P("stream", "span", None),
        P("stream", "span", None),
        P("stream", "span", None),
        P("stream", None),
        P("stream", None, None),
    )
    out_specs = (P("stream", "span", None), P("stream", "span", None), P())
    return jax.shard_map(local, mesh=mesh, in_specs=in_specs, out_specs=out_specs, check_vma=False)
```

time: 46.8 us -> 35.1 us (0.75)
  local copies, waits for them, and re-layouts: 6.74 us -> 0 us
  Pallas kernels: 39.1 us -> 34.4 us
    unnamed x16 -> x0, local copies, waits for them, and re-layouts: 6.23 us -> none
    pallas_call x1 -> x2, Pallas kernels: 39.1 us -> 34.4 us  [the longest x1 33.1 us: local(): pl.pallas_call(kernel, out_shape=(pltpu.VMEM(state.shape, F32), pltpu.VME...]
    squeeze x1 -> x0, local copies, waits for them, and re-layouts: 0.51 us -> none  [local(): return (res, bas, kry[0, :3])]
where the time goes in v1:
time: 35.1 us; the launch traced here: 35 us
  Pallas kernels  34.4 us (98%)
  between operations  0.64 us (2%)
    pallas_call x1, Pallas kernels, local(): pl.pallas_call(kernel, out_shape=(pltpu.VMEM(state.shape, F32), pltpu.VME...  33.1 us
    pallas_call x1, Pallas kernels, local(): pl.pallas_call(tail, out_shape=(pltpu.HBM(state.shape, F32), pltpu.HBM(st...  1.28 us

profile of v1, /device:TPU:1, one launch (start us, length us, event | category | flops | bytes accessed | tf_op | source)
XLA Modules:
  0.0 35.0 jit_solution(8102853681123846647)
XLA Ops:
  0.6 33.1 %hill.1 = (f32[40,2,625]{2,1,0:T(2,128)S(1)}, f32[40,2,625]{2,1,0:T(2,128)S(1)}, f32[1,128]{1,0:T(1,128)S(1)}) custom-call(f32[40,2,625]{2,1,0:T(2,128)} %state_in.1, f32[40,2,625]{2,1,0:T(2,128)} %dir_in.1, f32[3,2,40]{2,1,0:T(2,128)} %bitcast.3, s32[4,40]{1,0:T(4,128)} %bitcast.4, s32[2,33]{1,0:T(2,128)} %bitcast.5, bf16[384,384]{1,0:T(8,128)(2,1)} %constant.4.clone.op_in, ...), custom_call_target="tpu_custom_call" | custom-call | tf_op jit(solution)/shard_map/hill/pallas_call | solution.py:756
  33.7 1.3 %tail.1 = (f32[40,2,625]{2,1,0:T(2,128)}, f32[40,2,625]{2,1,0:T(2,128)}, f32[3]{0:T(128)}) custom-call(f32[40,2,625]{2,1,0:T(2,128)S(1)} %get-tuple-element.6.res_in, f32[40,2,625]{2,1,0:T(2,128)S(1)} %get-tuple-element.7.bas_in, f32[1,128]{1,0:T(1,128)S(1)} %get-tuple-element.8.kry_in), custom_call_target="tpu_custom_call" | custom-call | tf_op jit(solution)/shard_map/tail/pallas_call | solution.py:785

commit v2 on v1

--- a/solution.py
+++ b/solution.py
@@ -20,11 +20,18 @@
 LAYERS = 2
 ROWS = COLS * LAYERS
 SLOTS = 33
-SENT = 40
+SENT = 32
 CHUNK = 8
 STRIDES = (25, 5, 1)
+XY_ROWS = 2 * 2 * SLOTS
+Z_ROWS = 2 * 2 * COLS
 N_X, N_Z, N_SPAN = 4, 8, 4
 PLANE = 2 * N_X * N_SPAN
+FAR_PLANE = sorted(
+    ((i, j) for i in range(4) for j in range(4) if i or j),
+    key=lambda step: -min(step[0], 4 - step[0]) - min(step[1], 4 - step[1]),
+)
+FAR_Z = (4, 3, 5, 2, 6, 1, 7)
 
 
 def diff_table():
@@ -176,6 +183,10 @@
     sb2,
     rx1,
     rx2,
+    eb1,
+    eb2,
+    ex1,
+    ex2,
     rz1,
     rz2,
     g_s,
@@ -193,11 +204,39 @@
     pb_s,
     ar_a,
     ar_b,
+    ruler,
     xs_send,
     xs_recv,
     sum_sem,
     in_sem,
 ):
+    s = lax.axis_index("stream")
+    p = lax.axis_index("span")
+    n_s = 2 * N_X * N_Z
+    s_lo, s_hi = lax.rem(s + n_s - 1, n_s), lax.rem(s + 1, n_s)
+    p_lo, p_hi = lax.rem(p + N_SPAN - 1, N_SPAN), lax.rem(p + 1, N_SPAN)
+    core = lax.rem(p, 2)
+    x_at, z_at, y_hi, y_lo = s // (2 * N_Z), lax.rem(s // 2, N_Z), lax.rem(s, 2), p // 2
+    y_at = 2 * y_hi + y_lo
+    mine = 2 * (4 * x_at + y_at) + core
+
+    def plane_peer(i, j, c):
+        x, y = lax.rem(x_at + i, 4), lax.rem(y_at + j, 4)
+        return {"stream": x * (2 * N_Z) + 2 * z_at + y // 2, "span": 2 * lax.rem(y, 2) + c}
+
+    def column_peer(z, c):
+        return {"stream": x_at * (2 * N_Z) + 2 * z + y_hi, "span": 2 * y_lo + c}
+
+    barrier = pltpu.get_barrier_semaphore()
+
+    def greet(target):
+        pl.semaphore_signal(barrier, inc=1, device_id=target, device_id_type=MESH)
+
+    greet({"stream": s_lo, "span": p})
+    greet({"stream": s_hi, "span": p})
+    greet({"stream": s, "span": p_lo})
+    greet({"stream": s, "span": p_hi})
+
     loads = [
         pltpu.make_async_copy(src, dst, in_sem.at[i])
         for i, (src, dst) in enumerate(
@@ -215,42 +254,16 @@
     for load in loads:
         load.start()
 
-    s = lax.axis_index("stream")
-    p = lax.axis_index("span")
-    n_s = 2 * N_X * N_Z
-    s_lo, s_hi = lax.rem(s + n_s - 1, n_s), lax.rem(s + 1, n_s)
-    p_lo, p_hi = lax.rem(p + N_SPAN - 1, N_SPAN), lax.rem(p + 1, N_SPAN)
-    core = lax.rem(p, 2)
-    x_at, z_at, y_hi, y_lo = s // (2 * N_Z), lax.rem(s // 2, N_Z), lax.rem(s, 2), p // 2
-    chip = 4 * x_at + 2 * y_hi + y_lo
-    mine = 2 * chip + core
-
-    def plane_peer(j):
-        return {
-            "stream": (j // 8) * (2 * N_Z) + 2 * z_at + lax.rem(j // 4, 2),
-            "span": lax.rem(j, 4),
-        }
-
-    def column_peer(z, c):
-        return {"stream": x_at * (2 * N_Z) + 2 * z + y_hi, "span": 2 * y_lo + c}
-
-    barrier = pltpu.get_barrier_semaphore()
-
-    def greet(target):
-        pl.semaphore_signal(barrier, inc=1, device_id=target, device_id_type=MESH)
-
-    greet({"stream": s_lo, "span": p})
-    greet({"stream": s_hi, "span": p})
-    greet({"stream": s, "span": p_lo})
-    greet({"stream": s, "span": p_hi})
-
-    for k in range(1, N_Z):
+
+    for k in FAR_Z:
         greet(column_peer(lax.rem(z_at + k, N_Z), 1))
 
     @pl.when(core == 1)
     def _():
-        for k in range(1, PLANE):
-            greet(plane_peer(lax.rem(mine + k, PLANE)))
+        for i, j in FAR_PLANE:
+            greet(plane_peer(i, j, 0))
+            greet(plane_peer(i, j, 1))
+        greet(plane_peer(0, 0, 0))
 
     @pl.when(core == 0)
     def _():
@@ -275,10 +288,15 @@
                 moved = roll(field, v * stride)
                 lower = jnp.where(digit[axis] == float(v), moved, lower)
                 upper = jnp.where(over[axis] == float(v), moved, upper)
-        return roll(lower, 4 * stride), roll(upper, -4 * stride)
-
-    def pack_axis(fields, axis, pt, l, rc, faces):
+        return lower, upper
+
+    def settle(axis, up, value):
+        return roll(value, (-4 if up else 4) * STRIDES[axis])
+
+    def pack_axis(fields, axis, pt, l, rc, faces, settled):
         for up, value in enumerate(pack(fields, axis)):
+            if settled:
+                value = settle(axis, up, value)
             if axis < 2:
                 at = (2 * axis + up) * COLS + rc
                 tab_s[l, pl.ds(at, CHUNK), pt * 128 : pt * 128 + 128] = value
@@ -306,45 +324,52 @@
                 u_s[pt * 5 + v, pl.ds(row, CHUNK), :] = value
                 fields.append(value)
             for axis in range(3):
-                pack_axis(fields, axis, pt, l, rc, zp_s)
+                pack_axis(fields, axis, pt, l, rc, zp_s, True)
 
     def remote(src, dst, sem, target):
         return pltpu.make_async_remote_copy(
             src_ref=src,
             dst_ref=dst,
-            send_sem=xs_send.at[sem],
+            send_sem=xs_send.at[0],
             recv_sem=xs_recv.at[sem],
             device_id=target,
             device_id_type=MESH,
         )
 
+    def drain(count, sem):
+        part = ruler.at[pl.ds(0, count)]
+        pltpu.make_async_copy(part, part, sem).wait()
+
     def z_copies(faces, rz, base):
         return [
             remote(faces.at[0, 0], rz.at[1], base, {"stream": s, "span": p_lo}),
-            remote(faces.at[1, LAYERS - 1], rz.at[0], base + 1, {"stream": s, "span": p_hi}),
+            remote(faces.at[1, LAYERS - 1], rz.at[0], base, {"stream": s, "span": p_hi}),
         ]
 
-    def xy_copies(sb, rx, l, base):
+    def xy_copies(sb, rx, eb, ex, l, base):
         lower, upper = pl.ds(0, SENT), pl.ds(COLS, SENT)
+        below, above = {"stream": s_lo, "span": p}, {"stream": s_hi, "span": p}
+        base += 1 + l
         return [
-            remote(sb.at[l, lower], rx.at[l, upper], base + 2 + 2 * l, {"stream": s_lo, "span": p}),
-            remote(sb.at[l, upper], rx.at[l, lower], base + 3 + 2 * l, {"stream": s_hi, "span": p}),
+            remote(sb.at[l, lower], rx.at[l, upper], base, below),
+            remote(sb.at[l, upper], rx.at[l, lower], base, above),
+            remote(eb.at[l, 0], ex.at[l, 1], base, below),
+            remote(eb.at[l, 1], ex.at[l, 0], base, above),
         ]
 
     def start(copies):
         for copy in copies:
             copy.start()
 
-    def wait(copies):
-        for copy in copies:
-            copy.wait()
-
     def gather(hot, table):
         parts = split3(table)
         return dot(hot, parts[0]) + (dot(hot, parts[1]) + dot(hot, parts[2]))
 
-    def fill(sb, l):
-        sb[l] = gather(so_s[...], tab_s[l])
+    def fill(sb, eb, l):
+        value = gather(so_s[...], tab_s[l])
+        sb[l] = value
+        eb[l, 0] = value[SENT:SLOTS]
+        eb[l, 1] = value[COLS + SENT : COLS + SLOTS]
 
     with jax.named_scope("first0"):
         layer_loop(first, 0)
@@ -383,20 +408,20 @@
         )
         so_s[side * COLS : (side + 1) * COLS, :] = jnp.where(col == own_id, 1.0, 0.0).astype(BF16)
 
-    round1 = [xy_copies(sb1, rx1, l, 0) for l in range(LAYERS)]
+    round1 = [xy_copies(sb1, rx1, eb1, ex1, l, 0) for l in range(LAYERS)]
     round1_z = z_copies(zp_s, rz1, 0)
-    round2 = [xy_copies(sb2, rx2, l, 6) for l in range(LAYERS)]
-    round2_z = z_copies(zv_s, rz2, 6)
-
-    fill(sb1, 0)
+    round2 = [xy_copies(sb2, rx2, eb2, ex2, l, 3) for l in range(LAYERS)]
+    round2_z = z_copies(zv_s, rz2, 3)
+
+    fill(sb1, eb1, 0)
+    with jax.named_scope("first1"):
+        layer_loop(first, 1)
+        fill(sb1, eb1, 1)
     with jax.named_scope("barrier"):
         pl.semaphore_wait(barrier, 4 + 16 + 14 * core)
+    start(round1_z)
     start(round1[0])
-    with jax.named_scope("first1"):
-        layer_loop(first, 1)
-        start(round1_z)
-        fill(sb1, 1)
-        start(round1[1])
+    start(round1[1])
 
     for f in range(4):
         col = column(fs_ref[f : f + 1, :].astype(F32))
@@ -413,13 +438,15 @@
     def own_gather(l):
         g_s[l] = gather(oo_s[...], tab_s[l])
 
-    def far_gather(rx, l):
-        table = rx[l]
-        if SENT < COLS:
-            at = lax.broadcasted_iota(jnp.int32, (2 * COLS, 256), 0)
-            used = (at < SLOTS) | ((at >= COLS) & (at < COLS + SLOTS))
-            table = jnp.where(used, table, 0.0)
-        g_s[l] += gather(or_s[...], table)
+    def far_gather(rx, ex, l):
+        rx[l, SENT:SLOTS, :] = ex[l, 0]
+        rx[l, COLS + SENT : COLS + SLOTS, :] = ex[l, 1]
+        g_s[l] += gather(or_s[...], rx[l])
+
+    for rx in (rx1, rx2):
+        for l in range(LAYERS):
+            for side in range(2):
+                rx[l, side * COLS + SENT : (side + 1) * COLS, :] = jnp.zeros((COLS - SENT, 256), F32)
 
     def second(l, rc, row):
         u = [u_s[v, pl.ds(row, CHUNK), :] for v in range(10)]
@@ -494,18 +521,18 @@
             for pt, flux in enumerate((tau[a] + [energy], dtau[a] + [tangent])):
                 for i, value in enumerate(flux):
                     v_s[a, pt * 4 + i, here, :] = value
-                pack_axis(flux, a, pt, l, rc, zv_s)
+                pack_axis(flux, a, pt, l, rc, zv_s, False)
 
     with jax.named_scope("wait1z"):
-        wait(round1_z)
+        drain(Z_ROWS, xs_recv.at[0])
     for l in range(LAYERS):
         with jax.named_scope("wait1"):
-            wait(round1[l])
+            drain(XY_ROWS, xs_recv.at[1 + l])
         with jax.named_scope("third"):
-            far_gather(rx1, l)
+            far_gather(rx1, ex1, l)
             layer_loop(third, l)
             start(round2_z[l : l + 1])
-            fill(sb2, l)
+            fill(sb2, eb2, l)
             start(round2[l])
 
     def fourth(l, rc, row):
@@ -563,6 +590,7 @@
             side = m_s[a, here, :] * sgn[a]
             for pt in range(2):
                 pair = packed_pair(a, pt, l, rc, zv_s, rz2)
+                pair = [settle(a, 1, pair[0]), settle(a, 0, pair[1])]
                 for i in range(4):
                     value = unpack(pair, i, a, masks, v_s[a, pt * 4 + i, here, :])
                     total[pt * 5 + 1 + i] = total[pt * 5 + 1 + i] - side * value
@@ -583,12 +611,12 @@
             y_s[i, here, :] = total[i]
 
     with jax.named_scope("wait2z"):
-        wait(round2_z)
+        drain(Z_ROWS, xs_recv.at[3])
     for l in range(LAYERS):
         with jax.named_scope("wait2"):
-            wait(round2[l])
+            drain(XY_ROWS, xs_recv.at[4 + l])
         with jax.named_scope("fifth"):
-            far_gather(rx2, l)
+            far_gather(rx2, ex2, l)
             layer_loop(fifth, l)
 
     at = lax.broadcasted_iota(jnp.int32, (1, 128), 1)
@@ -596,13 +624,13 @@
     own = jnp.where(at == 0, own[0], jnp.where(at == 1, own[1], jnp.where(at == 2, own[2], own[3])))
     pt_s[...] = own
 
-    def to_plane(k):
+    def to_plane(i, j):
         return pltpu.make_async_remote_copy(
             src_ref=pt_s,
             dst_ref=ar_a.at[mine],
             send_sem=sum_sem.at[0],
             recv_sem=sum_sem.at[1],
-            device_id=plane_peer(2 * lax.rem(chip + k, PLANE // 2) + 1),
+            device_id=plane_peer(i, j, 1),
             device_id_type=MESH,
         )
 
@@ -616,16 +644,12 @@
             device_id_type=MESH,
         )
 
-    def drain(buffer, count, sem):
-        part = buffer.at[pl.ds(0, count)]
-        pltpu.make_async_copy(part, part, sum_sem.at[sem]).wait()
-
-    for k in range(1, PLANE // 2):
-        to_plane(k).start()
+    for i, j in FAR_PLANE:
+        to_plane(i, j).start()
 
     @pl.when(core == 0)
     def _():
-        to_plane(0).start()
+        to_plane(0, 0).start()
 
     @pl.when(core == 1)
     def _():
@@ -654,19 +678,19 @@
 
         @pl.when(core == 1)
         def _():
-            drain(ar_a, PLANE - 1, 1)
+            drain(PLANE - 1, sum_sem.at[1])
             total = jnp.sum(ar_a[...], axis=0)
             pb_s[...] = total
-            for k in range(1, N_Z):
+            for k in FAR_Z:
+                to_column(k, 0).start()
                 to_column(k, 1).start()
-                to_column(k, 0).start()
             to_column(0, 0).start()
             ar_b[z_at] = total
-            drain(ar_b, N_Z - 1, 3)
+            drain(N_Z - 1, sum_sem.at[3])
 
         @pl.when(core == 0)
         def _():
-            drain(ar_b, N_Z, 3)
+            drain(N_Z, sum_sem.at[3])
 
     sums = jnp.sum(ar_b[...], axis=0)
     dp_sum, dd_sum, rr_sum, pp_sum = [
@@ -685,25 +709,27 @@
         value = (x_out[1, part, :] - coefficient * x_s[1, part, :]) * scale
         bas_ref[:, l, :] = value[:, 0:625]
 
+    drain(2 * (LAYERS * XY_ROWS + Z_ROWS), xs_send.at[0])
+
     @pl.when(core == 0)
     def _():
-        drain(ar_a, PLANE // 2, 0)
+        drain(PLANE // 2, sum_sem.at[0])
 
     @pl.when(core == 1)
     def _():
-        drain(ar_a, PLANE // 2 - 1, 0)
-        drain(ar_a, 2 * N_Z - 1, 2)
-
-
-def tail(res_in, bas_in, kry_in, res_out, bas_out, kry_out, sem):
+        drain(PLANE // 2 - 1, sum_sem.at[0])
+        drain(2 * N_Z - 1, sum_sem.at[2])
+
+
+def tail(res_in, bas_in, kry_in, res_out, bas_out, kry_out, kry_s, sem):
+    kry_s[...] = kry_in[0, 0:3]
     copies = [
+        pltpu.make_async_copy(kry_s, kry_out, sem.at[2]),
         pltpu.make_async_copy(res_in, res_out, sem.at[0]),
         pltpu.make_async_copy(bas_in, bas_out, sem.at[1]),
     ]
     for copy in copies:
         copy.start()
-    for i in range(3):
-        kry_out[i] = jnp.sum(kry_in[0:1, i : i + 1])
     for copy in copies:
         copy.wait()
 
@@ -735,6 +761,10 @@
         ((LAYERS, 80, 256), F32),
         ((LAYERS, 80, 256), F32),
         ((LAYERS, 80, 256), F32),
+        ((LAYERS, 2, 1, 256), F32),
+        ((LAYERS, 2, 1, 256), F32),
+        ((LAYERS, 2, 1, 256), F32),
+        ((LAYERS, 2, 1, 256), F32),
         ((2, 2, COLS, 128), F32),
         ((2, 2, COLS, 128), F32),
         ((LAYERS, 160, 256), F32),
@@ -752,6 +782,7 @@
         ((1, 128), F32),
         ((PLANE, 1, 128), F32),
         ((N_Z, 1, 128), F32),
+        ((2 * (LAYERS * XY_ROWS + Z_ROWS), 1, 128), F32),
     ]
     res, bas, kry = pl.pallas_call(
         kernel,
@@ -763,7 +794,7 @@
         in_specs=[hbm] * 7,
         out_specs=(vmem, vmem, vmem),
         scratch_shapes=[pltpu.VMEM(shape, dtype) for shape, dtype in shapes]
-        + [pltpu.SemaphoreType.DMA((n,)) for n in (12, 12, 4, 7)],
+        + [pltpu.SemaphoreType.DMA((n,)) for n in (1, 6, 4, 7)],
         compiler_params=pltpu.CompilerParams(
             collective_id=0, has_side_effects=True, vmem_limit_bytes=48 * 1024 * 1024
         ),
@@ -787,11 +818,11 @@
         out_shape=(
             pltpu.HBM(state.shape, F32),
             pltpu.HBM(state.shape, F32),
-            jax.ShapeDtypeStruct((3,), F32),
+            pltpu.HBM((3,), F32),
         ),
         in_specs=[vmem] * 3,
-        out_specs=(hbm, hbm, pl.BlockSpec(memory_space=pltpu.SMEM)),
-        scratch_shapes=[pltpu.SemaphoreType.DMA((2,))],
+        out_specs=(hbm, hbm, hbm),
+        scratch_shapes=[pltpu.VMEM((3,), F32), pltpu.SemaphoreType.DMA((3,))],
         compiler_params=pltpu.CompilerParams(vmem_limit_bytes=1024 * 1024),
         name="tail",
     )(res, bas, kry)

time: 35.1 us -> 33.5 us (0.954)
  Pallas kernels: 34.4 us -> 32.8 us
    pallas_call x1, Pallas kernels: 33.1 us -> 32 us  [local(): pl.pallas_call(kernel, out_shape=(pltpu.VMEM(state.shape, F32), pltpu.VME...]
    pallas_call x1, Pallas kernels: 1.28 us -> 0.78 us  [local(): pl.pallas_call(tail, out_shape=(pltpu.HBM(state.shape, F32), pltpu.HBM(st...]
where the time goes in v2:
time: 33.5 us; the launch traced here: 33.4 us
  Pallas kernels  32.8 us (98%)
  between operations  0.64 us (2%)
    pallas_call x1, Pallas kernels, local(): pl.pallas_call(kernel, out_shape=(pltpu.VMEM(state.shape, F32), pltpu.VME...  32 us
    pallas_call x1, Pallas kernels, local(): pl.pallas_call(tail, out_shape=(pltpu.HBM(state.shape, F32), pltpu.HBM(st...  0.78 us

profile of v2, /device:TPU:1, one launch (start us, length us, event | category | flops | bytes accessed | tf_op | source)
XLA Modules:
  0.0 33.4 jit_solution(14914028850288632043)
XLA Ops:
  0.6 32.0 %hill.1 = (f32[40,2,625]{2,1,0:T(2,128)S(1)}, f32[40,2,625]{2,1,0:T(2,128)S(1)}, f32[1,128]{1,0:T(1,128)S(1)}) custom-call(f32[40,2,625]{2,1,0:T(2,128)} %state_in.1, f32[40,2,625]{2,1,0:T(2,128)} %dir_in.1, f32[3,2,40]{2,1,0:T(2,128)} %bitcast.3, s32[4,40]{1,0:T(4,128)} %bitcast.4, s32[2,33]{1,0:T(2,128)} %bitcast.5, bf16[384,384]{1,0:T(8,128)(2,1)} %constant.4.clone.op_in, ...), custom_call_target="tpu_custom_call" | custom-call | tf_op jit(solution)/shard_map/hill/pallas_call | solution.py:787
  32.7 0.8 %tail.1 = (f32[40,2,625]{2,1,0:T(2,128)}, f32[40,2,625]{2,1,0:T(2,128)}, f32[3]{0:T(128)}) custom-call(f32[40,2,625]{2,1,0:T(2,128)S(1)} %get-tuple-element.6.res_in, f32[40,2,625]{2,1,0:T(2,128)S(1)} %get-tuple-element.7.bas_in, f32[1,128]{1,0:T(1,128)S(1)} %get-tuple-element.8.kry_in), custom_call_target="tpu_custom_call" | custom-call | tf_op jit(solution)/shard_map/tail/pallas_call | solution.py:816
